TPU v7x, 32 devices: a whole 2x2x4 slice. The times are simulated.
32 devices in a mesh: section: 4 (over y, core), dp: 8 (over z, x).
Axes of the slice: x: 2, y: 2, z: 4, core: 2. Of those that a mesh axis runs over, the one named last changes fastest.
Arguments:
- section_inputs: bfloat16 [4, 2, 1024, 1024], P('section', None, 'dp'), may hold values from -6 to 6
- gain: float32 [4, 1024], P('section'), may hold values from 0.25 to 1.75
- w_gate: bfloat16 [4, 1024, 1536], P('section'), may hold values from -0.1875 to 0.1875
- w_up: bfloat16 [4, 1024, 1536], P('section'), may hold values from -0.1875 to 0.1875
- w_out: bfloat16 [4, 1024, 1536], P('section'), may hold values from -0.15625 to 0.15625
- out_grad: bfloat16 [2, 1024, 1024], P(None, 'dp'), may hold values from -6 to 6
Outputs:
- grad_w_gate: float32 [4, 1024, 1536], P('section', 'dp')
- grad_w_up: float32 [4, 1024, 1536], P('section', 'dp')
- grad_w_out: float32 [4, 1024, 1536], P('section', 'dp')
- grad_gain: float32 [4, 1024], P('section', 'dp')
- input_grads: bfloat16 [4, 2, 1024, 1024], P('section', None, 'dp')
All inputs are finite; a program needn't handle non-finite values.
Results may differ from a plain program's by a relative error of at most 0.014.
Values may be sent and summed in bfloat16 or wider, within the bound.
A program may use at most 128 MiB of HBM per device.

v0:
```python
import jax
import jax.numpy as jnp
from jax import lax
from jax.sharding import PartitionSpec as P

C_GELU = 0.7978845608028654
EPSILON = 1e-06


def from_behind(value, axis, steps):
    count = lax.axis_size(axis)
    leading, last = (max(0, -steps), min(count, count - steps))
    return lax.ppermute(value, axis, [(source, source + steps) for source in range(leading, last)])


def gelu_parts(pre_act):
    cubic = 0.044715 * pre_act * pre_act * pre_act
    tangent = jnp.tanh(C_GELU * (pre_act + cubic))
    gelu_value = 0.5 * pre_act * (1.0 + tangent)
    gelu_slope = 0.5 * (1.0 + tangent) + 0.5 * pre_act * (1.0 - tangent * tangent) * C_GELU * (
        1.0 + 3.0 * 0.044715 * pre_act * pre_act
    )
    return (gelu_value, gelu_slope)


def section_back(inputs_row, incoming, gain_row, w_gate_mat, w_up_mat, w_out_mat):
    inputs_float = inputs_row.astype(jnp.float32)
    inverse_rms = lax.rsqrt(jnp.mean(inputs_float * inputs_float, axis=-1, keepdims=True) + EPSILON)
    normed = (inputs_float * inverse_rms * gain_row).astype(jnp.bfloat16)
    gate_pre = jnp.dot(normed, w_gate_mat, preferred_element_type=jnp.float32)
    up_pre = jnp.dot(normed, w_up_mat, preferred_element_type=jnp.float32)
    gelu_value, gelu_slope = gelu_parts(gate_pre)
    hidden_act = (gelu_value * up_pre).astype(jnp.bfloat16)
    act_grad = jnp.dot(incoming, w_out_mat, preferred_element_type=jnp.float32)
    gate_grad = (act_grad * up_pre * gelu_slope).astype(jnp.bfloat16)
    up_grad = (act_grad * gelu_value).astype(jnp.bfloat16)
    transpose_dims = (((1,), (1,)), ((), ()))
    normed_grad = lax.dot_general(
        gate_grad, w_gate_mat, transpose_dims, preferred_element_type=jnp.float32
    )
    normed_grad = normed_grad + lax.dot_general(
        up_grad, w_up_mat, transpose_dims, preferred_element_type=jnp.float32
    )
    gain_term = jnp.sum(normed_grad * inputs_float * inverse_rms, axis=0)
    scaled_grad = normed_grad * gain_row
    input_grad = inverse_rms * scaled_grad - inputs_float * inverse_rms**3 * jnp.mean(
        scaled_grad * inputs_float, axis=-1, keepdims=True
    )
    passed = (incoming.astype(jnp.float32) + input_grad).astype(jnp.bfloat16)
    return (passed, hidden_act, gate_grad, up_grad, normed, gain_term)


def local(section_inputs, gain, w_gate, w_up, w_out, out_grad):
    section_count = lax.axis_size("section")
    position = lax.axis_index("section")
    inputs_here = section_inputs[0]
    gain_row = gain[0]
    w_gate_mat = w_gate[0]
    w_up_mat = w_up[0]
    w_out_mat = w_out[0]
    micro_count, tok_rows, model_width = inputs_here.shape
    hidden_width = w_gate_mat.shape[1]
    token_scale = 1.0 / (micro_count * tok_rows)

    def backward(inputs_row, incoming):
        return section_back(inputs_row, incoming, gain_row, w_gate_mat, w_up_mat, w_out_mat)

    narrow_rows = jnp.zeros((micro_count, tok_rows, model_width), jnp.bfloat16)
    wide_rows = jnp.zeros((micro_count, tok_rows, hidden_width), jnp.bfloat16)
    store = (
        narrow_rows,
        wide_rows,
        wide_rows,
        wide_rows,
        narrow_rows,
        narrow_rows,
        jnp.zeros((model_width,), jnp.float32),
    )

    def run_all(operand):
        incoming_all, previous = operand
        results = [
            backward(inputs_here[member], incoming_all[member]) for member in range(micro_count)
        ]
        gain_sum = results[0][5]
        member = 1
        gain_sum = gain_sum + results[member][5]
        stacked = tuple((jnp.stack([result[index] for result in results]) for index in range(5)))
        return stacked + (incoming_all, gain_sum)

    incoming_all = out_grad
    for section_level in reversed(range(section_count)):
        store = lax.cond(
            position == section_level, run_all, lambda operand: operand[1], (incoming_all, store)
        )
        if section_level > 0:
            incoming_all = from_behind(store[0], "section", -1)
    hidden_flat = store[1].reshape(-1, hidden_width)
    gate_flat = store[2].reshape(-1, hidden_width)
    up_flat = store[3].reshape(-1, hidden_width)
    normed_flat = store[4].reshape(-1, model_width)
    incoming_flat = store[5].reshape(-1, model_width)
    contract = (((0,), (0,)), ((), ()))
    gate_part = lax.dot_general(
        normed_flat, gate_flat, contract, preferred_element_type=jnp.float32
    )
    up_part = lax.dot_general(normed_flat, up_flat, contract, preferred_element_type=jnp.float32)
    out_part = lax.dot_general(
        incoming_flat, hidden_flat, contract, preferred_element_type=jnp.float32
    )
    all_rows = lax.psum_scatter(
        jnp.concatenate([gate_part, up_part, out_part], axis=1) * token_scale,
        "dp",
        scatter_dimension=0,
        tiled=True,
    )
    gate_rows = all_rows[:, :hidden_width]
    up_rows = all_rows[:, hidden_width : 2 * hidden_width]
    out_rows = all_rows[:, 2 * hidden_width :]
    gain_rows = lax.psum_scatter(store[6] * token_scale, "dp", scatter_dimension=0, tiled=True)
    return (gate_rows[None], up_rows[None], out_rows[None], gain_rows[None], store[0][None])


def solution(mesh):
    placed = (
        P("section", None, "dp", None),
        P("section", None),
        P("section", None, None),
        P("section", None, None),
        P("section", None, None),
        P(None, "dp", None),
    )
    return jax.shard_map(
        local,
        mesh=mesh,
        in_specs=placed,
        out_specs=(
            P("section", "dp", None),
            P("section", "dp", None),
            P("section", "dp", None),
            P("section", "dp"),
            P("section", None, "dp", None),
        ),
        check_vma=False,
    )
```

profile of v0, /device:TPU:0, one launch (start us, length us, event | category | flops | bytes accessed | tf_op | source)
XLA Modules:
  0.0 424.5 jit_solution(10434999368195522594)
XLA Ops:
  7.2 1.0 copy.78
  8.3 2.0 conditional.4
  10.3 1.3 collective-permute-start
  11.6 2.7 collective-permute-done
  14.3 1.3 collective-permute-start.1
  15.6 10.3 %collective-permute-done.1 = bf16[2,128,1024]{2,1,0:T(8,128)(2,1)S(1)} collective-permute-done((bf16[2,128,1024]{2,1,0:T(8,128)(2,1)}, bf16[2,128,1024]{2,1,0:T(8,128)(2,1)S(1)}, u32[]{:S(2)}, u32[]{:S(2)}) %collective-permute-start.1) | collective-permute-done | bytes 524320 | tf_op jit(solution)/shard_map/ppermute | solution.py:13
  25.9 1.3 collective-permute-start.2
  27.2 50.0 %collective-permute-done.2 = bf16[2,128,1024]{2,1,0:T(8,128)(2,1)S(1)} collective-permute-done((bf16[2,128,1024]{2,1,0:T(8,128)(2,1)}, bf16[2,128,1024]{2,1,0:T(8,128)(2,1)S(1)}, u32[]{:S(2)}, u32[]{:S(2)}) %collective-permute-start.2) | collective-permute-done | bytes 524320 | tf_op jit(solution)/shard_map/ppermute | solution.py:13
  77.2 16.0 %conditional.7 = (bf16[2,128,1536]{2,1,0:T(8,128)(2,1)}, bf16[2,128,1536]{2,1,0:T(8,128)(2,1)S(1)}, bf16[2,128,1536]{2,1,0:T(8,128)(2,1)S(1)}, bf16[2,128,1024]{...) conditional(s32[]{:T(128)} %convert_element_type.252, ...), branch_computations={%region_24.0_spmd, %region_25.0_spmd} | conditional | flops 4046454272 | bytes 99432648 | solution.py:93
  77.2 1.4 fusion.222
  78.6 1.4 fusion.233
  81.5 1.3 copy-done.19
  82.8 1.0 multiply_convert_fusion.12
  83.8 1.1 fusion.287
  84.9 1.1 convolution_add_fusion.6
  87.3 1.0 multiply_convert_fusion.13
  89.5 1.1 fusion.286
  90.6 1.3 fusion.231
  94.2 1.0 convolution_bitcast_fusion.1
  95.2 2.2 convolution_bitcast_fusion
  97.4 6.9 %maximum_multiply_fusion = f32[1024,4608]{1,0:T(8,128)} fusion(f32[1024,1536]{1,0:T(8,128)S(1)} %convolution_bitcast_fusion, f32[1024,1536]{1,0:T(8,128)S(1)} %convolution_bitcast_fusion.1, f32[1024,1536]{1,0:T(8,128)S(1)} %convolution_bitcast_fusion.2), kind=kLoop, calls=%fused_computation.356 | loop fusion | flops 14155776 | bytes 37748736 | tf_op jit(solution)/shard_map/mul | solution.py:112
  106.2 22.8 %all-reduce = f32[1024]{0:T(1024)S(1)} all-reduce(f32[1024]{0:T(1024)S(1)} %broadcast_multiply_fusion.8), channel_id=3, replica_groups=mesh['section'=4,'dp'=8] {'dp'}, use_global_device_ids=true, to_apply=%region_33.0.clone | all-reduce | flops 1024 | bytes 8192
  129.5 285.0 %reduce-scatter.2.cloned.1.call-done = f32[128,4608]{1,0:T(8,128)} async-done(((f32[1024,4608]{1,0:T(8,128)}), f32[128,4608]{1,0:T(8,128)}) %reduce-scatter.2.cloned.1.call-update) | async-done | bytes 2359312 | tf_op jit(solution)/shard_map/reduce_scatter | solution.py:111
  414.6 3.1 slice_bitcast_fusion
  (41 shorter events, 10.0 us)
Async XLA Ops:
  7.2 407.4 %reduce-scatter.2.cloned.1.call-start = ((), (), s32[]{:S(2)}) async-start(), calls=%async_computation.1 | async-start | bytes 21233664 | tf_op jit(solution)/shard_map/reduce_scatter | solution.py:111
  10.3 4.0 collective-permute-start
  14.3 11.6 %collective-permute-start.1 = (bf16[2,128,1024]{2,1,0:T(8,128)(2,1)}, bf16[2,128,1024]{2,1,0:T(8,128)(2,1)S(1)}, u32[]{:S(2)}, u32[]{:S(2)}) collective-permute-start(bf16[2,128,1024]{2,1,0:T(8,128)(2,1)} %get-tuple-element.151), channel_id=1, source_target_pairs={{8,0},{16,8},{24,16},{9,1},{17,9},{25,17},{10,2},{18,10},{26,18},{... | collective-permute-start | bytes 1572872 | tf_op jit(solution)/shard_map/ppermute | solution.py:13
  25.9 51.3 %collective-permute-start.2 = (bf16[2,128,1024]{2,1,0:T(8,128)(2,1)}, bf16[2,128,1024]{2,1,0:T(8,128)(2,1)S(1)}, u32[]{:S(2)}, u32[]{:S(2)}) collective-permute-start(bf16[2,128,1024]{2,1,0:T(8,128)(2,1)} %get-tuple-element.339), channel_id=1, source_target_pairs={{8,0},{16,8},{24,16},{9,1},{17,9},{25,17},{10,2},{18,10},{26,18},{... | collective-permute-start | bytes 1572872 | tf_op jit(solution)/shard_map/ppermute | solution.py:13
  77.2 2.9 copy-start.3
  77.2 2.9 copy-start.11
  77.2 2.9 copy-start.15
  78.6 2.3 copy-start.7
  80.9 1.9 copy-start.19
  104.3 0.7 copy-start.20
Sparse Core Ops, SparseCore 0:
  104.4 310.1 reduce-scatter.1
where the time goes:
time: 425 us; the launch traced here: 424 us
  waiting for transfers between devices  348 us (82%)
  blocking collectives  22.8 us (5%)
  between operations  14.7 us (3%)
  matrix products  13.5 us (3%)
  other arithmetic  12 us (3%)
  local copies, waits for them, and re-layouts  9.34 us (2%)
    reduce_scatter x1, waiting for transfers between devices, local(): lax.psum_scatter(jnp.concatenate([gate_part, up_part, out_part], axis=1)...  285 us
    ppermute x3, waiting for transfers between devices, from_behind(): lax.ppermute(value, axis, [(source, source + steps) for source in range(l...  63 us
    unnamed x1, blocking collectives  22.8 us
  transfers between devices with their start and end apart: 4, of which 4 were waited for; matrix products, arithmetic and copies ran while one was open for 0% of the time, Pallas kernels for 0%

commit v1 on v0

--- a/solution.py
+++ b/solution.py
@@ -50,7 +50,7 @@
     return (passed, hidden_act, gate_grad, up_grad, normed, gain_term)
 
 
-def local(section_inputs, gain, w_gate, w_up, w_out, out_grad):
+def local_scatter(section_inputs, gain, w_gate, w_up, w_out, out_grad):
     section_count = lax.axis_size("section")
     position = lax.axis_index("section")
     inputs_here = section_inputs[0]
@@ -121,6 +121,101 @@
     return (gate_rows[None], up_rows[None], out_rows[None], gain_rows[None], store[0][None])
 
 
+def forward_parts(rows, gain_row, w_gate_mat, w_up_mat):
+    rows_float = rows.astype(jnp.float32)
+    inverse_rms = lax.rsqrt(jnp.mean(rows_float * rows_float, axis=-1, keepdims=True) + EPSILON)
+    normed = (rows_float * inverse_rms * gain_row).astype(jnp.bfloat16)
+    gate_pre = jnp.dot(normed, w_gate_mat, preferred_element_type=jnp.float32)
+    up_pre = jnp.dot(normed, w_up_mat, preferred_element_type=jnp.float32)
+    gelu_value, gelu_slope = gelu_parts(gate_pre)
+    hidden_act = (gelu_value * up_pre).astype(jnp.bfloat16)
+    gate_factor = (up_pre * gelu_slope).astype(jnp.bfloat16)
+    up_factor = gelu_value.astype(jnp.bfloat16)
+    return (inverse_rms, normed, hidden_act, gate_factor, up_factor)
+
+
+def local_gather(section_inputs, gain, w_gate, w_up, w_out, out_grad):
+    section_count = lax.axis_size("section")
+    position = lax.axis_index("section")
+    replica = lax.axis_index("dp")
+    replicas = lax.axis_size("dp")
+    gain_row = gain[0]
+    w_gate_mat = w_gate[0]
+    w_up_mat = w_up[0]
+    w_out_mat = w_out[0]
+    _, micro_count, tok_rows, model_width = section_inputs.shape
+    rows_own = micro_count * tok_rows
+    token_scale = 1.0 / rows_own
+    row_count = model_width // replicas
+    rows = section_inputs[0].reshape(rows_own, model_width)
+    rows_all = lax.all_gather(rows, "dp", axis=0, tiled=True)
+    inverse_rms, _, _, gate_factor, up_factor = forward_parts(rows, gain_row, w_gate_mat, w_up_mat)
+    transpose_dims = (((1,), (1,)), ((), ()))
+
+    def stage(operand):
+        incoming, _ = operand
+        act_grad = jnp.dot(incoming, w_out_mat, preferred_element_type=jnp.float32)
+        gate_grad = (act_grad * gate_factor).astype(jnp.bfloat16)
+        up_grad = (act_grad * up_factor).astype(jnp.bfloat16)
+        normed_grad = lax.dot_general(
+            gate_grad, w_gate_mat, transpose_dims, preferred_element_type=jnp.float32
+        ) + lax.dot_general(up_grad, w_up_mat, transpose_dims, preferred_element_type=jnp.float32)
+        rows_float = rows.astype(jnp.float32)
+        gain_term = jnp.sum(normed_grad * rows_float * inverse_rms, axis=0)
+        scaled_grad = normed_grad * gain_row
+        input_grad = inverse_rms * scaled_grad - rows_float * inverse_rms**3 * jnp.mean(
+            scaled_grad * rows_float, axis=-1, keepdims=True
+        )
+        passed = (incoming.astype(jnp.float32) + input_grad).astype(jnp.bfloat16)
+        return (passed, incoming, gain_term)
+
+    incoming = out_grad.reshape(rows_own, model_width)
+    store = (
+        jnp.zeros((rows_own, model_width), jnp.bfloat16),
+        jnp.zeros((rows_own, model_width), jnp.bfloat16),
+        jnp.zeros((model_width,), jnp.float32),
+    )
+    for level in reversed(range(section_count)):
+        store = lax.cond(
+            position == level, stage, lambda operand: operand[1], (incoming, store)
+        )
+        if level > 0:
+            incoming = lax.ppermute(store[0], "section", [(level, level - 1)])
+    passed, incoming, gain_term = store
+    incoming_all = lax.all_gather(incoming, "dp", axis=0, tiled=True)
+    gain_all = lax.all_gather(gain_term, "dp", axis=0)
+    _, normed_all, hidden_all, gate_factor_all, up_factor_all = forward_parts(
+        rows_all, gain_row, w_gate_mat, w_up_mat
+    )
+    act_all = jnp.dot(incoming_all, w_out_mat, preferred_element_type=jnp.float32)
+    gate_all = (act_all * gate_factor_all).astype(jnp.bfloat16)
+    up_all = (act_all * up_factor_all).astype(jnp.bfloat16)
+    own = replica * row_count
+    normed_own = lax.dynamic_slice_in_dim(normed_all, own, row_count, axis=1)
+    incoming_own = lax.dynamic_slice_in_dim(incoming_all, own, row_count, axis=1)
+    contract = (((0,), (0,)), ((), ()))
+
+    def grad_rows(left, right):
+        total = lax.dot_general(left, right, contract, preferred_element_type=jnp.float32)
+        return (total * token_scale)[None]
+
+    gain_rows = lax.dynamic_slice_in_dim(gain_all, own, row_count, axis=1).sum(axis=0)
+    return (
+        grad_rows(normed_own, gate_all),
+        grad_rows(normed_own, up_all),
+        grad_rows(incoming_own, hidden_all),
+        (gain_rows * token_scale)[None],
+        passed.reshape(section_inputs.shape),
+    )
+
+
+def local(section_inputs, gain, w_gate, w_up, w_out, out_grad):
+    _, micro_count, tok_rows, _ = section_inputs.shape
+    gathered_rows = lax.axis_size("dp") * micro_count * tok_rows
+    plan = local_gather if 2 * gathered_rows <= 3 * w_gate.shape[2] else local_scatter
+    return plan(section_inputs, gain, w_gate, w_up, w_out, out_grad)
+
+
 def solution(mesh):
     placed = (
         P("section", None, "dp", None),

time: 425 us -> 211 us (0.50)
  waiting for transfers between devices: 348 us -> 75.7 us
  matrix products: 13.5 us -> 67.8 us
  blocking collectives: 22.8 us -> 31.4 us
    reduce_scatter x1 -> x0, waiting for transfers between devices: 285 us -> none  [local(): lax.psum_scatter(jnp.concatenate([gate_part, up_part, out_part], axis=1)...]
    dot_general x13 -> x11, matrix products: 13.5 us -> 67.8 us  [the longest x3 29.5 us: grad_rows(): lax.dot_general(left, right, contract, preferred_element_type=jnp.float32)]
    all_gather x0 -> x2, waiting for transfers between devices: none -> 41.6 us  [the longest x1 41.6 us: local_gather(): incoming_all = lax.all_gather(incoming, 'dp', axis=0, tiled=True)]
    all_gather x0 -> x1, blocking collectives: none -> 31.4 us  [local_gather(): gain_all = lax.all_gather(gain_term, 'dp', axis=0)]
    ppermute x3, waiting for transfers between devices: 63 us -> 33.4 us  [local_gather(): incoming = lax.ppermute(store[0], 'section', [(level, level - 1)])]
    unnamed x1 -> x0, blocking collectives: 22.8 us -> none
    mul x2 -> x1, other arithmetic: 6.86 us -> 0.52 us  [local_gather(): gain_rows * token_scale]
    unnamed x4 -> x26, local copies, waits for them, and re-layouts: 2.25 us -> 7.93 us
  transfers between devices with their start and end apart: 4 -> 5, of which waited for: 4 -> 2; matrix products, arithmetic and copies ran while one was open for 0% -> 18% of each run, Pallas kernels for 0% -> 0%
where the time goes in v1:
time: 211 us; the launch traced here: 210 us
  waiting for transfers between devices  75.7 us (36%)
  matrix products  67.8 us (32%)
  blocking collectives  31.4 us (15%)
  between operations  14.3 us (7%)
  local copies, waits for them, and re-layouts  9.73 us (5%)
  other arithmetic  8.75 us (4%)
  starting transfers between devices  2.74 us (1%)
    all_gather x1, waiting for transfers between devices, local_gather(): incoming_all = lax.all_gather(incoming, 'dp', axis=0, tiled=True)  41.6 us
    ppermute x3, waiting for transfers between devices, local_gather(): incoming = lax.ppermute(store[0], 'section', [(level, level - 1)])  33.4 us
    all_gather x1, blocking collectives, local_gather(): gain_all = lax.all_gather(gain_term, 'dp', axis=0)  31.4 us
    dot_general x3, matrix products, grad_rows(): lax.dot_general(left, right, contract, preferred_element_type=jnp.float32)  29.5 us
    dot_general x2, matrix products, forward_parts(): gate_pre = jnp.dot(normed, w_gate_mat, preferred_element_type=jnp.float32)  12.5 us
    dot_general x2, matrix products, forward_parts(): up_pre = jnp.dot(normed, w_up_mat, preferred_element_type=jnp.float32)  10.9 us
    dot_general x1, matrix products, local_gather(): jnp.dot(incoming_all, w_out_mat, preferred_element_type=jnp.float32)  9.5 us
    unnamed x26, local copies, waits for them, and re-layouts  7.93 us
  transfers between devices with their start and end apart: 5, of which 2 were waited for; matrix products, arithmetic and copies ran while one was open for 18% of the time, Pallas kernels for 0%

profile of v1, /device:TPU:0, one launch (start us, length us, event | category | flops | bytes accessed | tf_op | source)
XLA Modules:
  0.0 210.4 jit_solution(2766487330108355180)
XLA Ops:
  8.0 1.2 fusion.59
  9.2 1.2 fusion.61
  10.4 3.3 %multiply_convert_fusion.34 = (bf16[256,1536]{1,0:T(8,128)(2,1)S(1)}, f32[256,1536]{1,0:T(8,128)S(1)}) fusion(bf16[256,1024]{1,0:T(8,128)(2,1)S(1)} %bitcast.81, bf16[1,1024,1536]{2,1,0:T(8,128)(2,1)} %param.16), kind=kOutput, calls=%fused_computation.101 | convolution fusion | flops 808845312 | bytes 6029312 | tf_op jit(solution)/shard_map/dot_general | solution.py:128
  13.8 1.5 fusion.47
  15.8 1.0 copy-done.6
  16.8 0.9 conditional.4
  19.2 1.3 collective-permute-start.2
  20.5 33.4 %collective-permute-done.2 = bf16[256,1024]{1,0:T(8,128)(2,1)S(1)} collective-permute-done((bf16[256,1024]{1,0:T(8,128)(2,1)}, bf16[256,1024]{1,0:T(8,128)(2,1)S(1)}, u32[]{:S(2)}, u32[]{:S(2)}) %collective-permute-start.2) | collective-permute-done | bytes 524320 | tf_op jit(solution)/shard_map/ppermute | solution.py:183
  53.9 7.5 %conditional.7 = (bf16[256,1024]{1,0:T(8,128)(2,1)S(1)}, f32[1024]{0:T(1024)S(1)}, bf16[1,2,128,1024]{3,2,1,0:T(8,128)(2,1)}) conditional(s32[]{:T(128)} %convert_element_type.144, (bf16[256,1024]{1,0:T(8,128)(2,1)S(1)}, f32[1024]{0:T(1024)S(1)}, bf16[256,1024]{1,0:T(8,128)(2,1)}) %tuple.66, (bf16[256,1024]{1,0:T(8,128)(2,1)S(1)}, ...), branch_computations={%region_14.15_spmd, %region_15.18_spmd} | conditional | flops 2422734336 | bytes 48780368 | solution.py:179
  53.9 3.0 %fusion.93 = f32[256,1536]{1,0:T(8,128)S(1)} fusion(bf16[256,1024]{1,0:T(8,128)(2,1)S(1)} %get-tuple-element.193, bf16[1024,1536]{1,0:T(8,128)(2,1)} %get-tuple-element.125), kind=kOutput, calls=%fused_computation.142 | convolution fusion | flops 805306368 | bytes 5242880 | tf_op jit(solution)/shard_map/cond/branch_1_fun/dot_general | solution.py:157
  56.9 1.0 fusion.31
  58.8 1.3 fusion.30
  60.1 1.2 fusion.29
  62.1 31.4 %all-gather = f32[8192]{0:T(1024)S(1)} all-gather(f32[1024]{0:T(1024)S(1)} %get-tuple-element.152), channel_id=2, replica_groups=mesh['section'=4,'dp'=8] {'dp'}, dimensions={0}, use_global_device_ids=true | all-gather | bytes 36864 | tf_op jit(solution)/shard_map/all_gather | solution.py:186
  94.1 3.5 %fusion.39 = f32[2048]{0:T(1024)S(1)} fusion(bf16[2048,1024]{1,0:T(8,128)(2,1)} %all-gather.4.cloned.1.call-done), kind=kLoop, calls=%fused_computation.79 | loop fusion | flops 6289408 | bytes 4202496 | tf_op jit(solution)/shard_map/reduce_sum | solution.py:126
  98.0 1.1 fusion.41
  99.8 9.3 %fusion.68 = f32[2048,1536]{1,0:T(8,128)} fusion(bf16[2048,1024]{1,0:T(8,128)(2,1)S(1)} %fusion.41, bf16[1,1024,1536]{2,1,0:T(8,128)(2,1)S(1)} %copy-done.2), kind=kOutput, calls=%fused_computation.117 | convolution fusion | flops 6442450944 | bytes 19922944 | tf_op jit(solution)/shard_map/dot_general | solution.py:128
  109.1 9.4 %fusion.72 = f32[2048,1536]{1,0:T(8,128)} fusion(bf16[2048,1024]{1,0:T(8,128)(2,1)S(1)} %fusion.41, bf16[1,1024,1536]{2,1,0:T(8,128)(2,1)S(1)} %copy-done.8), kind=kOutput, calls=%fused_computation.121 | convolution fusion | flops 6442450944 | bytes 19922944 | tf_op jit(solution)/shard_map/dot_general | solution.py:129
  118.5 41.6 %all-gather.6.cloned.1.call-done = bf16[2048,1024]{1,0:T(8,128)(2,1)} async-done(((bf16[256,1024]{1,0:T(8,128)(2,1)}), bf16[2048,1024]{1,0:T(8,128)(2,1)}) %all-gather.6.cloned.1.call-update) | async-done | bytes 4194320 | tf_op jit(solution)/shard_map/all_gather | solution.py:185
  160.1 9.5 %fusion.75 = f32[2048,1536]{1,0:T(8,128)S(1)} fusion(bf16[2048,1024]{1,0:T(8,128)(2,1)} %all-gather.6.cloned.1.call-done, bf16[1,1024,1536]{2,1,0:T(8,128)(2,1)} %param.18), kind=kOutput, calls=%fused_computation.124 | convolution fusion | flops 6442450944 | bytes 19922944 | tf_op jit(solution)/shard_map/dot_general | solution.py:190
  169.6 4.5 %copy-done.18 = f32[2048,1536]{1,0:T(8,128)} copy-done((f32[2048,1536]{1,0:T(8,128)}, f32[2048,1536]{1,0:T(8,128)S(1)}, u32[]{:S(2)}) %copy-start.18) | copy-done | bytes 12582936
  174.1 7.2 %fusion.51 = f32[1,128,1536]{2,1,0:T(8,128)} fusion(f32[2048,1536]{1,0:T(8,128)S(1)} %fusion.75, f32[2048,1536]{1,0:T(8,128)S(1)} %copy-done.17, bf16[2048,1024]{1,0:T(8,128)(2,1)} %copy-done.15, s32[]{:T(128)S(6)} %select_n.2), kind=kOutput, calls=%fused_computation.91 | convolution fusion | flops 843251712 | bytes 26476548 | tf_op jit(solution)/shard_map/dot_general | solution.py:199
  181.3 13.8 %fusion.53 = f32[1,128,1536]{2,1,0:T(8,128)} fusion(f32[2048,1536]{1,0:T(8,128)} %copy-done.18, f32[2048,1536]{1,0:T(8,128)} %fusion.72, f32[2048,1536]{1,0:T(8,128)S(1)} %copy-done.17, bf16[2048,1024]{1,0:T(8,128)(2,1)} %copy-done.15, s32[]{:T(128)S(6)} %select_n.2), kind=kOutput, calls=%fused_computation.93 | convolution fusion | flops 874708992 | bytes 39059460 | tf_op jit(solution)/shard_map/dot_general | solution.py:199
  195.0 8.6 %fusion.49 = f32[1,128,1536]{2,1,0:T(8,128)} fusion(f32[2048,1536]{1,0:T(8,128)} %fusion.72, f32[2048,1536]{1,0:T(8,128)S(1)} %copy-done.17, bf16[2048,1024]{1,0:T(8,128)(2,1)} %all-gather.6.cloned.1.call-done, s32[]{:T(128)S(6)} %select_n.2), kind=kOutput, calls=%fused_computation.89 | convolution fusion | flops 836960256 | bytes 26476548 | tf_op jit(solution)/shard_map/dot_general | solution.py:199
  (50 shorter events, 7.0 us)
Async XLA Ops:
  7.2 86.9 %all-gather.4.cloned.1.call-start = ((), (), s32[]{:S(2)}) async-start(), calls=%async_computation | async-start | bytes 4718592 | tf_op jit(solution)/shard_map/all_gather | solution.py:151
  7.9 152.2 %all-gather.6.cloned.1.call-start = ((), (), s32[]{:S(2)}) async-start(), calls=%async_computation.1 | async-start | bytes 4718592 | tf_op jit(solution)/shard_map/all_gather | solution.py:185
  10.4 3.3 %copy-start.7 = (bf16[1,1024,1536]{2,1,0:T(8,128)(2,1)S(1)}, bf16[1,1024,1536]{2,1,0:T(8,128)(2,1)}, u32[]{:S(2)}) copy-start(bf16[1,1024,1536]{2,1,0:T(8,128)(2,1)} %param.17) | copy-start | bytes 9437188
  13.7 1.6 copy-start
  13.7 2.1 copy-start.1
  13.8 3.0 %copy-start.6 = (bf16[1,1024,1536]{2,1,0:T(8,128)(2,1)S(1)}, bf16[1,1024,1536]{2,1,0:T(8,128)(2,1)}, u32[]{:S(2)}) copy-start(bf16[1,1024,1536]{2,1,0:T(8,128)(2,1)} %param.18) | copy-start | bytes 9437188
  13.8 3.0 %copy-start.14 = (bf16[2,128,1024]{2,1,0:T(8,128)(2,1)S(1)}, bf16[2,128,1024]{2,1,0:T(8,128)(2,1)}, u32[]{:S(2)}) copy-start(bf16[2,128,1024]{2,1,0:T(8,128)(2,1)} %param.19) | copy-start | bytes 1572868
  13.8 3.0 %copy-start.16 = (f32[1,1024]{1,0:T(1,128)S(1)}, f32[1,1024]{1,0:T(1,128)}, u32[]{:S(2)}) copy-start(f32[1,1024]{1,0:T(1,128)} %param.15) | copy-start | bytes 12292
  17.7 0.7 collective-permute-start
  18.4 0.7 collective-permute-start.1
  19.2 34.7 %collective-permute-start.2 = (bf16[256,1024]{1,0:T(8,128)(2,1)}, bf16[256,1024]{1,0:T(8,128)(2,1)S(1)}, u32[]{:S(2)}, u32[]{:S(2)}) collective-permute-start(bf16[256,1024]{1,0:T(8,128)(2,1)} %get-tuple-element.198), channel_id=1, source_target_pairs={{8,0},{9,1},{10,2},{11,3},{12,4},{13,5},{14,6},{15,7}} | collective-permute-start | bytes 1572872 | tf_op jit(solution)/shard_map/ppermute | solution.py:183
  53.9 3.1 %copy-start.5 = (bf16[1024,1536]{1,0:T(8,128)(2,1)S(1)}, bf16[1024,1536]{1,0:T(8,128)(2,1)}, u32[]{:S(2)}) copy-start(bf16[1024,1536]{1,0:T(8,128)(2,1)} %get-tuple-element.127) | copy-start | bytes 9437188 | tf_op jit(solution)/shard_map/cond
  56.9 1.9 copy-start.11
  61.3 0.8 copy-start.13
  94.1 3.9 %copy-start.12 = (bf16[2048,1024]{1,0:T(8,128)(2,1)S(1)}, bf16[2048,1024]{1,0:T(8,128)(2,1)}, u32[]{:S(2)}) copy-start(bf16[2048,1024]{1,0:T(8,128)(2,1)} %all-gather.4.cloned.1.call-done) | copy-start | bytes 12582916
  98.0 1.9 copy-start.2
  99.8 9.3 %copy-start.15 = (bf16[2048,1024]{1,0:T(8,128)(2,1)}, bf16[2048,1024]{1,0:T(8,128)(2,1)S(1)}, u32[]{:S(2)}) copy-start(bf16[2048,1024]{1,0:T(8,128)(2,1)S(1)} %fusion.41) | copy-start | bytes 12582916
  99.8 9.3 %copy-start.8 = (bf16[1,1024,1536]{2,1,0:T(8,128)(2,1)S(1)}, bf16[1,1024,1536]{2,1,0:T(8,128)(2,1)}, u32[]{:S(2)}) copy-start(bf16[1,1024,1536]{2,1,0:T(8,128)(2,1)} %param.17) | copy-start | bytes 9437188
  160.1 14.0 %copy-start.17 = (f32[2048,1536]{1,0:T(8,128)S(1)}, f32[2048,1536]{1,0:T(8,128)}, u32[]{:S(2)}) copy-start(f32[2048,1536]{1,0:T(8,128)} %fusion.68) | copy-start | bytes 37748740
  169.6 4.5 %copy-start.18 = (f32[2048,1536]{1,0:T(8,128)}, f32[2048,1536]{1,0:T(8,128)S(1)}, u32[]{:S(2)}) copy-start(f32[2048,1536]{1,0:T(8,128)S(1)} %fusion.75) | copy-start | bytes 37748740
Sparse Core Ops, SparseCore 0:
  10.1 75.9 all-gather.3
  88.8 71.2 all-gather.5

commit v2 on v1

--- a/solution.py
+++ b/solution.py
@@ -1,6 +1,8 @@
 import jax
 import jax.numpy as jnp
 from jax import lax
+from jax.experimental import pallas as pl
+from jax.experimental.pallas import tpu as pltpu
 from jax.sharding import PartitionSpec as P
 
 C_GELU = 0.7978845608028654
@@ -132,6 +134,69 @@
     gate_factor = (up_pre * gelu_slope).astype(jnp.bfloat16)
     up_factor = gelu_value.astype(jnp.bfloat16)
     return (inverse_rms, normed, hidden_act, gate_factor, up_factor)
+
+
+def grad_kernel(token_scale, g_ref, normed_ref, hidden_ref, gate_ref, up_ref, wo_ref, *rest):
+    sums = rest
+
+    @pl.when(pl.program_id(0) == 0)
+    def _():
+        for target in sums:
+            target[...] = jnp.zeros_like(target)
+
+    row_count = sums[0].shape[0]
+    hidden_width = wo_ref.shape[1]
+    own = pl.ds(pl.multiple_of(lax.axis_index("dp") * row_count, row_count), row_count)
+    incoming = g_ref[...]
+    incoming_own = g_ref[:, own]
+    normed_own = normed_ref[...]
+    chunk = 512 if hidden_width % 512 == 0 else hidden_width
+
+    def add_rows(target, columns, left, right):
+        term = lax.dot_general(
+            left, right, (((0,), (0,)), ((), ())), preferred_element_type=jnp.float32
+        )
+        target[:, columns] += term * token_scale
+
+    for start in range(0, hidden_width, chunk):
+        columns = slice(start, start + chunk)
+        act_grad = jnp.dot(incoming, wo_ref[:, columns], preferred_element_type=jnp.float32)
+        gate_grad = (act_grad * gate_ref[:, columns].astype(jnp.float32)).astype(jnp.bfloat16)
+        up_grad = (act_grad * up_ref[:, columns].astype(jnp.float32)).astype(jnp.bfloat16)
+        add_rows(sums[0], columns, normed_own, gate_grad)
+        add_rows(sums[1], columns, normed_own, up_grad)
+        add_rows(sums[2], columns, incoming_own, hidden_ref[:, columns])
+
+
+def grad_rows_of(incoming, normed_own, hidden, gate_factor, up_factor, w_out_mat, token_scale):
+    rows, model_width = incoming.shape
+    hidden_width = w_out_mat.shape[1]
+    row_count = normed_own.shape[1]
+    block = 256 if rows % 256 == 0 else rows
+
+    def tokens(width):
+        return pl.BlockSpec((block, width), lambda i: (i, 0))
+
+    def fixed(shape):
+        return pl.BlockSpec(shape, lambda i: (0, 0))
+
+    total = fixed((row_count, hidden_width))
+    return pl.pallas_call(
+        lambda *refs: grad_kernel(token_scale, *refs),
+        name="grad_rows",
+        grid=(rows // block,),
+        in_specs=[tokens(model_width), tokens(row_count)]
+        + [tokens(hidden_width)] * 3
+        + [fixed((model_width, hidden_width))],
+        out_specs=[total] * 3,
+        out_shape=[jax.ShapeDtypeStruct((row_count, hidden_width), jnp.float32)] * 3,
+        compiler_params=pltpu.CompilerParams(vmem_limit_bytes=40 * 1024 * 1024),
+        cost_estimate=pl.CostEstimate(
+            flops=2 * rows * (model_width + 3 * row_count) * hidden_width,
+            bytes_accessed=6 * rows * hidden_width + 12 * row_count * hidden_width,
+            transcendentals=0,
+        ),
+    )(incoming, normed_own, hidden, gate_factor, up_factor, w_out_mat)
 
 
 def local_gather(section_inputs, gain, w_gate, w_up, w_out, out_grad):
@@ -167,43 +232,33 @@
             scaled_grad * rows_float, axis=-1, keepdims=True
         )
         passed = (incoming.astype(jnp.float32) + input_grad).astype(jnp.bfloat16)
-        return (passed, incoming, gain_term)
+        return (passed, gain_term)
 
     incoming = out_grad.reshape(rows_own, model_width)
     store = (
         jnp.zeros((rows_own, model_width), jnp.bfloat16),
-        jnp.zeros((rows_own, model_width), jnp.bfloat16),
         jnp.zeros((model_width,), jnp.float32),
     )
     for level in reversed(range(section_count)):
-        store = lax.cond(
-            position == level, stage, lambda operand: operand[1], (incoming, store)
-        )
+        store = lax.cond(position == level, stage, lambda operand: operand[1], (incoming, store))
         if level > 0:
-            incoming = lax.ppermute(store[0], "section", [(level, level - 1)])
-    passed, incoming, gain_term = store
+            received = lax.ppermute(store[0], "section", [(level, level - 1)])
+            incoming = jnp.where(position == level - 1, received, incoming)
+    passed, gain_sum = store
+
     incoming_all = lax.all_gather(incoming, "dp", axis=0, tiled=True)
-    gain_all = lax.all_gather(gain_term, "dp", axis=0)
-    _, normed_all, hidden_all, gate_factor_all, up_factor_all = forward_parts(
-        rows_all, gain_row, w_gate_mat, w_up_mat
-    )
-    act_all = jnp.dot(incoming_all, w_out_mat, preferred_element_type=jnp.float32)
-    gate_all = (act_all * gate_factor_all).astype(jnp.bfloat16)
-    up_all = (act_all * up_factor_all).astype(jnp.bfloat16)
     own = replica * row_count
-    normed_own = lax.dynamic_slice_in_dim(normed_all, own, row_count, axis=1)
-    incoming_own = lax.dynamic_slice_in_dim(incoming_all, own, row_count, axis=1)
-    contract = (((0,), (0,)), ((), ()))
-
-    def grad_rows(left, right):
-        total = lax.dot_general(left, right, contract, preferred_element_type=jnp.float32)
-        return (total * token_scale)[None]
-
+    _, normed, hidden, gate_all, up_all = forward_parts(rows_all, gain_row, w_gate_mat, w_up_mat)
+    normed_own = lax.dynamic_slice_in_dim(normed, own, row_count, axis=1)
+    sums = grad_rows_of(
+        incoming_all, normed_own, hidden, gate_all, up_all, w_out_mat, token_scale
+    )
+    gain_all = lax.all_gather(gain_sum, "dp", axis=0)
     gain_rows = lax.dynamic_slice_in_dim(gain_all, own, row_count, axis=1).sum(axis=0)
     return (
-        grad_rows(normed_own, gate_all),
-        grad_rows(normed_own, up_all),
-        grad_rows(incoming_own, hidden_all),
+        sums[0][None],
+        sums[1][None],
+        sums[2][None],
         (gain_rows * token_scale)[None],
         passed.reshape(section_inputs.shape),
     )
@@ -212,7 +267,8 @@
 def local(section_inputs, gain, w_gate, w_up, w_out, out_grad):
     _, micro_count, tok_rows, _ = section_inputs.shape
     gathered_rows = lax.axis_size("dp") * micro_count * tok_rows
-    plan = local_gather if 2 * gathered_rows <= 3 * w_gate.shape[2] else local_scatter
+    small = lax.axis_size("dp") % 2 == 0 and 2 * gathered_rows <= 3 * w_gate.shape[2]
+    plan = local_gather if small else local_scatter
     return plan(section_inputs, gain, w_gate, w_up, w_out, out_grad)
 
 

time: 211 us -> 191 us (0.905)
  matrix products: 67.8 us -> 33 us
  Pallas kernels: 0 us -> 18.2 us
  waiting for transfers between devices: 75.7 us -> 70.6 us
    dot_general x4 -> x0, matrix products: 39 us -> none  [the longest x3 29.5 us: grad_rows(): lax.dot_general(left, right, contract, preferred_element_type=jnp.float32)]
    pallas_call x0 -> x1, Pallas kernels: none -> 18.2 us  [grad_rows_of(): pl.pallas_call(lambda *refs: grad_kernel(token_scale, *refs), name='grad_...]
    dot_general x2, matrix products: 10.9 us -> 17.4 us  [forward_parts(): up_pre = jnp.dot(normed, w_up_mat, preferred_element_type=jnp.float32)]
    all_gather x1, waiting for transfers between devices: 41.6 us -> 36.4 us  [local_gather(): incoming_all = lax.all_gather(incoming, 'dp', axis=0, tiled=True)]
    dot_general x2, matrix products: 12.5 us -> 9.99 us  [forward_parts(): gate_pre = jnp.dot(normed, w_gate_mat, preferred_element_type=jnp.float32)]
    unnamed x26 -> x24, local copies, waits for them, and re-layouts: 7.93 us -> 7.34 us
  transfers between devices with their start and end apart: 5 -> 5, of which waited for: 2 -> 2; matrix products, arithmetic and copies ran while one was open for 18% -> 23% of each run, Pallas kernels for 0% -> 0%
where the time goes in v2:
time: 191 us; the launch traced here: 190 us
  waiting for transfers between devices  70.6 us (37%)
  matrix products  33 us (17%)
  blocking collectives  31.5 us (16%)
  Pallas kernels  18.2 us (10%)
  between operations  14.2 us (7%)
  other arithmetic  9.67 us (5%)
  local copies, waits for them, and re-layouts  8.39 us (4%)
  starting transfers between devices  4.3 us (2%)
    all_gather x1, waiting for transfers between devices, local_gather(): incoming_all = lax.all_gather(incoming, 'dp', axis=0, tiled=True)  36.4 us
    ppermute x3, waiting for transfers between devices, local_gather(): received = lax.ppermute(store[0], 'section', [(level, level - 1)])  33.5 us
    all_gather x1, blocking collectives, local_gather(): gain_all = lax.all_gather(gain_sum, 'dp', axis=0)  31.5 us
    pallas_call x1, Pallas kernels, grad_rows_of(): pl.pallas_call(lambda *refs: grad_kernel(token_scale, *refs), name='grad_...  18.2 us
    dot_general x2, matrix products, forward_parts(): up_pre = jnp.dot(normed, w_up_mat, preferred_element_type=jnp.float32)  17.4 us
    dot_general x2, matrix products, forward_parts(): gate_pre = jnp.dot(normed, w_gate_mat, preferred_element_type=jnp.float32)  9.99 us
    unnamed x24, local copies, waits for them, and re-layouts  7.34 us
    reduce_sum x2, other arithmetic, forward_parts(): jnp.mean(rows_float * rows_float, axis=-1, keepdims=True) + EPSILON  4.6 us
  transfers between devices with their start and end apart: 5, of which 2 were waited for; matrix products, arithmetic and copies ran while one was open for 23% of the time, Pallas kernels for 0%

profile of v2, /device:TPU:0, one launch (start us, length us, event | category | flops | bytes accessed | tf_op | source)
XLA Modules:
  0.0 190.2 jit_solution(10545530735151291325)
XLA Ops:
  8.0 1.2 fusion.49
  9.2 1.2 fusion.51
  10.4 3.3 %multiply_convert_fusion.17 = (bf16[256,1536]{1,0:T(8,128)(2,1)S(1)}, f32[256,1536]{1,0:T(8,128)S(1)}) fusion(bf16[256,1024]{1,0:T(8,128)(2,1)S(1)} %bitcast.79, bf16[1,1024,1536]{2,1,0:T(8,128)(2,1)} %param.16), kind=kOutput, calls=%fused_computation.90 | convolution fusion | flops 808845312 | bytes 6029312 | tf_op jit(solution)/shard_map/dot_general | solution.py:130
  13.8 1.5 fusion.43
  15.8 1.0 copy-done.8
  16.9 1.5 collective-permute-start
  18.5 1.5 collective-permute-start.1
  20.0 1.3 collective-permute-start.2
  21.3 33.5 %collective-permute-done.2 = bf16[256,1024]{1,0:T(8,128)(2,1)S(1)} collective-permute-done((bf16[256,1024]{1,0:T(8,128)(2,1)}, bf16[256,1024]{1,0:T(8,128)(2,1)S(1)}, u32[]{:S(2)}, u32[]{:S(2)}) %collective-permute-start.2) | collective-permute-done | bytes 524320 | tf_op jit(solution)/shard_map/ppermute | solution.py:245
  54.8 0.8 broadcast_select_fusion.2
  55.7 7.8 %conditional.7 = (f32[1024]{0:T(1024)S(1)}, bf16[1,2,128,1024]{3,2,1,0:T(8,128)(2,1)}) conditional(s32[]{:T(128)} %convert_element_type.143, (f32[1024]{0:T(1024)S(1)}, bf16[256,1024]{1,0:T(8,128)(2,1)}) %tuple.68, (bf16[256,1024]{1,0:T(8,128)(2,1)}, bf16[1024,1536]{1,0:T(8,128)(2,1)}, bf16[256,1536]{1,0:T(8,128)(2,1)S(1)}, ...), branch_computations={%region_14.15_spmd, %region_15.18_spmd} | conditional | flops 2422734336 | bytes 49828964 | solution.py:243
  55.9 3.2 %fusion.62 = f32[256,1536]{1,0:T(8,128)S(1)} fusion(bf16[256,1024]{1,0:T(8,128)(2,1)} %get-tuple-element.116, bf16[1024,1536]{1,0:T(8,128)(2,1)} %get-tuple-element.117), kind=kOutput, calls=%fused_computation.114 | convolution fusion | flops 805306368 | bytes 5242880 | tf_op jit(solution)/shard_map/cond/branch_1_fun/dot_general | solution.py:222
  59.1 1.0 fusion.31
  61.0 1.3 fusion.30
  62.3 1.2 fusion.29
  63.5 31.5 %all-gather = f32[8192]{0:T(1024)S(1)} all-gather(f32[1024]{0:T(1024)S(1)} %get-tuple-element.146), channel_id=2, replica_groups=mesh['section'=4,'dp'=8] {'dp'}, dimensions={0}, use_global_device_ids=true | all-gather | bytes 36864 | tf_op jit(solution)/shard_map/all_gather | solution.py:256
  95.6 3.4 %fusion.39 = f32[2048]{0:T(1024)S(1)} fusion(bf16[2048,1024]{1,0:T(8,128)(2,1)} %all-gather.6.cloned.1.call-done), kind=kLoop, calls=%fused_computation.77 | loop fusion | flops 6289408 | bytes 4202496 | tf_op jit(solution)/shard_map/reduce_sum | solution.py:128
  99.2 1.1 fusion.41
  101.1 6.7 %fusion.52 = f32[2048,1536]{1,0:T(8,128)S(1)} fusion(bf16[2048,1024]{1,0:T(8,128)(2,1)S(1)} %fusion.41, bf16[1,1024,1536]{2,1,0:T(8,128)(2,1)S(1)} %copy-done.4), kind=kOutput, calls=%fused_computation.104 | convolution fusion | flops 6442450944 | bytes 19922944 | tf_op jit(solution)/shard_map/dot_general | solution.py:130
  107.8 15.9 %fusion.38 = (bf16[2048,1536]{1,0:T(8,128)(2,1)}, bf16[2048,1536]{1,0:T(8,128)(2,1)}, bf16[2048,1536]{1,0:T(8,128)(2,1)}) fusion(f32[2048,1536]{1,0:T(8,128)S(1)} %fusion.52, bf16[2048,1024]{1,0:T(8,128)(2,1)S(1)} %fusion.41, bf16[1,1024,1536]{2,1,0:T(8,128)(2,1)S(1)} %copy-done.10), kind=kOutput, calls=%fused_computation.72 | convolution fusion | flops 6514802688 | bytes 38797312 | tf_op jit(solution)/shard_map/dot_general | solution.py:131
  123.8 36.4 %all-gather.4.cloned.1.call-done.refs_0_ = bf16[2048,1024]{1,0:T(8,128)(2,1)} async-done(((bf16[256,1024]{1,0:T(8,128)(2,1)}), bf16[2048,1024]{1,0:T(8,128)(2,1)}) %all-gather.4.cloned.1.call-update) | async-done | bytes 4194320 | tf_op jit(solution)/shard_map/all_gather | solution.py:249
  160.2 2.2 %copy-done = bf16[2048,1024]{1,0:T(8,128)(2,1)S(1)} copy-done((bf16[2048,1024]{1,0:T(8,128)(2,1)S(1)}, bf16[2048,1024]{1,0:T(8,128)(2,1)}, u32[]{:S(2)}) %copy-start) | copy-done | bytes 4194328
  162.4 2.8 %copy-done.1 = bf16[2048,1536]{1,0:T(8,128)(2,1)S(1)} copy-done((bf16[2048,1536]{1,0:T(8,128)(2,1)S(1)}, bf16[2048,1536]{1,0:T(8,128)(2,1)}, u32[]{:S(2)}) %copy-start.1) | copy-done | bytes 6291480
  165.1 18.2 %grad_rows.1 = (f32[128,1536]{1,0:T(8,128)}, f32[128,1536]{1,0:T(8,128)}, f32[128,1536]{1,0:T(8,128)}) custom-call(bf16[2048,1024]{1,0:T(8,128)(2,1)S(1)} %copy-done, bf16[2048,128]{1,0:T(8,128)(2,1)S(1)} %constant_dynamic-slice_fusion.refs_1_, bf16[2048,1536]{1,0:T(8,128)(2,1)S(1)} %copy-done.1, bf16[2048,1536]{1,0:T(8,128)(2,1)} %get-tuple-element.163.refs_3_, ...), custom_call_target="tpu_custom_call" | custom-call | flops 8858370048 | bytes 21233664 | tf_op jit(solution)/shard_map/grad_rows/pallas_call | solution.py:184
  (49 shorter events, 4.0 us)
Async XLA Ops:
  7.2 88.4 %all-gather.6.cloned.1.call-start = ((), (), s32[]{:S(2)}) async-start(), calls=%async_computation.1 | async-start | bytes 4718592 | tf_op jit(solution)/shard_map/all_gather | solution.py:216
  7.9 152.3 %all-gather.4.cloned.1.call-start = ((), (), s32[]{:S(2)}) async-start(), calls=%async_computation | async-start | bytes 4718592 | tf_op jit(solution)/shard_map/all_gather | solution.py:249
  10.4 3.3 %copy-start.9 = (bf16[1,1024,1536]{2,1,0:T(8,128)(2,1)S(1)}, bf16[1,1024,1536]{2,1,0:T(8,128)(2,1)}, u32[]{:S(2)}) copy-start(bf16[1,1024,1536]{2,1,0:T(8,128)(2,1)} %param.17) | copy-start | bytes 9437188
  13.7 1.6 copy-start.2
  13.7 2.1 %copy-start.3 = (bf16[1,1024,1536]{2,1,0:T(8,128)(2,1)S(1)}, bf16[1,1024,1536]{2,1,0:T(8,128)(2,1)}, u32[]{:S(2)}) copy-start(bf16[1,1024,1536]{2,1,0:T(8,128)(2,1)} %param.16) | copy-start | bytes 9437188
  13.8 3.0 %copy-start.8 = (bf16[1,1024,1536]{2,1,0:T(8,128)(2,1)S(1)}, bf16[1,1024,1536]{2,1,0:T(8,128)(2,1)}, u32[]{:S(2)}) copy-start(bf16[1,1024,1536]{2,1,0:T(8,128)(2,1)} %param.18) | copy-start | bytes 9437188
  13.8 3.0 %copy-start.16 = (bf16[2,128,1024]{2,1,0:T(8,128)(2,1)S(1)}, bf16[2,128,1024]{2,1,0:T(8,128)(2,1)}, u32[]{:S(2)}) copy-start(bf16[2,128,1024]{2,1,0:T(8,128)(2,1)} %param.19) | copy-start | bytes 1572868
  13.8 3.0 %copy-start.18 = (f32[1,1024]{1,0:T(1,128)S(1)}, f32[1,1024]{1,0:T(1,128)}, u32[]{:S(2)}) copy-start(f32[1,1024]{1,0:T(1,128)} %param.15) | copy-start | bytes 12292
  16.9 1.5 copy-start.17
  16.9 1.5 collective-permute-start
  18.5 1.5 collective-permute-start.1
  20.0 34.8 %collective-permute-start.2 = (bf16[256,1024]{1,0:T(8,128)(2,1)}, bf16[256,1024]{1,0:T(8,128)(2,1)S(1)}, u32[]{:S(2)}, u32[]{:S(2)}) collective-permute-start(bf16[256,1024]{1,0:T(8,128)(2,1)} %get-tuple-element.185), channel_id=1, source_target_pairs={{8,0},{9,1},{10,2},{11,3},{12,4},{13,5},{14,6},{15,7}} | collective-permute-start | bytes 1572872 | tf_op jit(solution)/shard_map/ppermute | solution.py:245
  55.9 3.2 %copy-start.7 = (bf16[1024,1536]{1,0:T(8,128)(2,1)S(1)}, bf16[1024,1536]{1,0:T(8,128)(2,1)}, u32[]{:S(2)}) copy-start(bf16[1024,1536]{1,0:T(8,128)(2,1)} %get-tuple-element.119) | copy-start | bytes 9437188 | tf_op jit(solution)/shard_map/cond
  59.1 1.9 copy-start.13
  61.0 1.3 copy-start.15
  95.6 3.6 %copy-start.14 = (bf16[2048,1024]{1,0:T(8,128)(2,1)S(1)}, bf16[2048,1024]{1,0:T(8,128)(2,1)}, u32[]{:S(2)}) copy-start(bf16[2048,1024]{1,0:T(8,128)(2,1)} %all-gather.6.cloned.1.call-done) | copy-start | bytes 12582916
  99.2 1.9 copy-start.4
  101.1 6.7 %copy-start.10 = (bf16[1,1024,1536]{2,1,0:T(8,128)(2,1)S(1)}, bf16[1,1024,1536]{2,1,0:T(8,128)(2,1)}, u32[]{:S(2)}) copy-start(bf16[1,1024,1536]{2,1,0:T(8,128)(2,1)} %param.17) | copy-start | bytes 9437188
  160.2 2.2 %copy-start = (bf16[2048,1024]{1,0:T(8,128)(2,1)S(1)}, bf16[2048,1024]{1,0:T(8,128)(2,1)}, u32[]{:S(2)}) copy-start(bf16[2048,1024]{1,0:T(8,128)(2,1)} %all-gather.4.cloned.1.call-done.refs_0_) | copy-start | bytes 12582916
  162.4 2.8 %copy-start.1 = (bf16[2048,1536]{1,0:T(8,128)(2,1)S(1)}, bf16[2048,1536]{1,0:T(8,128)(2,1)}, u32[]{:S(2)}) copy-start(bf16[2048,1536]{1,0:T(8,128)(2,1)} %get-tuple-element.164.refs_2_) | copy-start | bytes 18874372
Sparse Core Ops, SparseCore 0:
  10.1 75.9 all-gather.5
  88.8 71.3 all-gather.3
